TPU v7x, 256 devices: a whole 4x4x8 slice. The times are simulated.
256 devices in a mesh: edge: 64 (over y, z, x_lo), chan: 4 (over x_hi, core).
Axes of the slice: x: 4 (x_hi: 2, x_lo: 2; x = x_hi * 2 + x_lo), y: 4, z: 8, core: 2. Of those that a mesh axis runs over, the one named last changes fastest.
Arguments:
- node_states: bfloat16 [1024, 49, 256], P('edge', None, 'chan'), may hold values from -6 to 6
- edge_vectors: float32 [3, 32768], P(None, ('edge', 'chan')), may hold values from -5.6 to 5.6, as said below
- source_part: int32 [32768, 1], P('edge'), may hold values from 0 to 63; in each aligned block of 512 rows (0 to 511, 512 to 1023, ...) at most 16 rows name the same one
- source_slot: int32 [32768], P('edge'), may hold values from 0 to 15
- target_slot: int32 [32768], P('edge'), may hold values from 0 to 15
- live_edges: int32 [64], P('edge'), may hold values from 1 to 512, 24576 in all
- weight_zero: bfloat16 [7, 256, 7, 256], P(None, 'chan'), may hold values from -0.125 to 0.125
- weight_one: bfloat16 [2, 6, 256, 6, 256], P(None, None, 'chan'), may hold values from -0.109375 to 0.109375
- weight_two: bfloat16 [2, 5, 256, 5, 256], P(None, None, 'chan'), may hold values from -0.125 to 0.125
Outputs:
- aggregated: bfloat16 [1024, 49, 256], P('edge', None, 'chan')
Inputs may be any that keep to these rules, and one draw needn't show every extreme that they name: `source_part`: in each aligned block of 512 rows (the edges of one partition's slab) no partition number appears more than 16 times, and some number appears exactly 16 times. Edges are grouped by destination partition: the destination of an edge in slab p is node p * 16 + target_slot. `live_edges`: live slots stand at the front of each slab; the fullest slab is full. `edge_vectors`: every column has length between 0.8 and 5.6.
All inputs are finite; a program needn't handle non-finite values. No bound on the sum of `live_edges` on one device may be relied on, other than what follows from the above.
Results may differ from a plain program's by a relative error of at most 0.015.
Values may be sent and summed in bfloat16 or wider, within the bound.
A program may use at most 128 MiB of HBM per device.

v0:
```python
import math
import jax
import jax.numpy as jnp
import numpy as np
from jax import lax
from jax.sharding import PartitionSpec as P

LMAX = 6
MMAX = 2
cutoff_radius = 6.0
highest = lax.Precision.HIGHEST


def harmonics(coord_x, coord_y, coord_z, degree_top, order_top):
    results = {}
    real_part = [coord_x * 0.0 + 1.0]
    imag_part = [coord_x * 0.0]
    for azimuthal in range(1, order_top + 1):
        new_real = coord_x * real_part[-1] - coord_y * imag_part[-1]
        new_imag = coord_x * imag_part[-1] + coord_y * real_part[-1]
        real_part.append(new_real)
        imag_part.append(new_imag)
    for azimuthal in range(order_top + 1):
        start_value = (-1.0) ** azimuthal * math.prod(range(2 * azimuthal - 1, 0, -2))
        legendre = {azimuthal: coord_z * 0.0 + start_value}
        if azimuthal + 1 <= degree_top:
            legendre[azimuthal + 1] = coord_z * ((2 * azimuthal + 1) * start_value)
        for degree in range(azimuthal + 2, degree_top + 1):
            legendre[degree] = (
                (2 * degree - 1) * coord_z * legendre[degree - 1]
                - (degree + azimuthal - 1) * legendre[degree - 2]
            ) / (degree - azimuthal)
        for degree in range(azimuthal, degree_top + 1):
            factor = math.sqrt(
                (2 * degree + 1)
                / (4.0 * math.pi)
                * math.factorial(degree - azimuthal)
                / math.factorial(degree + azimuthal)
            )
            if azimuthal == 0:
                results[degree, 0] = factor * legendre[degree]
            else:
                results[degree, azimuthal] = (
                    math.sqrt(2.0) * factor * legendre[degree] * real_part[azimuthal]
                )
                results[degree, -azimuthal] = (
                    math.sqrt(2.0) * factor * legendre[degree] * imag_part[azimuthal]
                )
    return results


def kept_rows():
    row_list = [(degree, 0) for degree in range(LMAX + 1)]
    for azimuthal in range(1, MMAX + 1):
        row_list += [(degree, azimuthal) for degree in range(azimuthal, LMAX + 1)]
        row_list += [(degree, -azimuthal) for degree in range(azimuthal, LMAX + 1)]
    return row_list


def row_offsets():
    listing = []
    offset = 0
    for degree, azimuthal in kept_rows():
        listing.append((degree, offset))
        offset += 2 * degree + 1
    return listing


def invert_small(matrix):
    order_size = matrix.shape[0]
    work = np.concatenate([matrix, np.eye(order_size)], axis=1)
    for column in range(order_size):
        work[column] = work[column] / work[column, column]
        for row_index in range(order_size):
            if row_index != column:
                work[row_index] = work[row_index] - work[row_index, column] * work[column]
    return work[:, order_size:]


def sample_tables():
    sample_count = 2 * (LMAX + 1) ** 2
    positions = np.arange(sample_count) + 0.5
    height = 1.0 - 2.0 * positions / sample_count
    radius = np.sqrt(1.0 - height * height)
    azimuth = math.pi * (3.0 - math.sqrt(5.0)) * positions
    points = np.stack([radius * np.cos(azimuth), radius * np.sin(azimuth), height])
    values = harmonics(points[0], points[1], points[2], LMAX, LMAX)
    inverses = []
    for degree in range(LMAX + 1):
        sampled = np.stack([values[degree, azimuthal] for azimuthal in range(-degree, degree + 1)])
        inverses.append(sampled.T @ invert_small(sampled @ sampled.T))
    return (points, inverses)


def wigner_rows(vectors):
    length = jnp.sqrt(jnp.sum(vectors * vectors, axis=0))
    direction = vectors / length
    pick_first = jnp.where(jnp.abs(direction[0]) < 0.6, 1.0, 0.0).astype(jnp.float32)
    helper = jnp.stack([pick_first, 1.0 - pick_first, jnp.zeros_like(pick_first)])
    first_axis = jnp.cross(direction, helper, axis=0)
    first_axis = first_axis / jnp.sqrt(jnp.sum(first_axis * first_axis, axis=0))
    second_axis = jnp.cross(direction, first_axis, axis=0)
    frames = jnp.stack([first_axis, second_axis, direction])
    points, inverses = sample_tables()
    sample = jnp.asarray(points, jnp.float32)
    turned = jnp.einsum("rce,ck->rek", frames, sample, precision=highest)
    values = harmonics(turned[0], turned[1], turned[2], LMAX, MMAX)
    pieces = []
    for degree, azimuthal in kept_rows():
        table = jnp.asarray(inverses[degree], jnp.float32)
        pieces.append(jnp.dot(values[degree, azimuthal], table, precision=highest))
    compact = jnp.concatenate(pieces, axis=1)
    envelope = 0.5 * (jnp.cos(math.pi * length / cutoff_radius) + 1.0)
    return (compact, envelope)


def one_hot(indices, width):
    return (indices[:, None] == jnp.arange(width, dtype=jnp.int32)[None, :]).astype(jnp.bfloat16)


def rotate_forward(compact_t, scaling, sources):
    rows_out = []
    for degree, offset in row_offsets():
        span = 2 * degree + 1
        total = None
        for inner in range(span):
            term = compact_t[offset + inner].astype(jnp.float32)[None, :] * sources[
                degree * degree + inner
            ].astype(jnp.float32)
            total = term if total is None else total + term
        rows_out.append(total * scaling[None, :])
    return jnp.stack(rows_out, axis=0).astype(jnp.bfloat16)


def convolve(turned, weight_zero, weight_one, weight_two):
    end_zero = LMAX + 1
    end_one_plus = end_zero + LMAX
    end_one_minus = end_one_plus + LMAX
    end_two_plus = end_one_minus + LMAX - 1
    zero_part = turned[:end_zero]
    one_plus = turned[end_zero:end_one_plus]
    one_minus = turned[end_one_plus:end_one_minus]
    two_plus = turned[end_one_minus:end_two_plus]
    two_minus = turned[end_two_plus:]

    def contract(parts, weight, rows):
        left = jnp.concatenate(parts, axis=0)
        edges = left.shape[-1]
        left = left.reshape(-1, edges)
        right = weight.reshape(left.shape[0], -1)
        out = lax.dot_general(
            left, right, (((0,), (0,)), ((), ())), preferred_element_type=jnp.float32
        ).astype(jnp.bfloat16)
        return [out[:, row * 256 : (row + 1) * 256] for row in range(rows)]

    return (
        contract([zero_part], weight_zero, LMAX + 1)
        + contract([one_plus, -one_minus], weight_one, LMAX)
        + contract([one_minus, one_plus], weight_one, LMAX)
        + contract([two_plus, -two_minus], weight_two, LMAX - 1)
        + contract([two_minus, two_plus], weight_two, LMAX - 1)
    )


def shards(
    node_states,
    edge_vectors,
    source_part,
    source_slot,
    target_slot,
    live_edges,
    weight_zero,
    weight_one,
    weight_two,
):
    slab_size = source_slot.shape[0]
    local_nodes = node_states.shape[0]
    local_channels = node_states.shape[2]
    coef_count = node_states.shape[1]
    group_count = lax.axis_size("edge")
    node_flat = node_states.reshape(local_nodes, coef_count * local_channels)
    table = lax.all_gather(node_flat, "edge", axis=0, tiled=True)
    quarter, quarter_fade = wigner_rows(edge_vectors)
    packed = jnp.concatenate([quarter, quarter_fade[:, None]], axis=1).astype(jnp.bfloat16)
    packed_t = lax.all_gather(packed, "chan", axis=0, tiled=True).T
    compact_t, envelope = (packed_t[:-1], packed_t[-1])
    alive_mask = (jnp.arange(slab_size, dtype=jnp.int32) < live_edges[0]).astype(jnp.float32)
    scaling = envelope.astype(jnp.float32) * alive_mask
    source = source_part[:, 0] * local_nodes + source_slot
    select = one_hot(source, group_count * local_nodes)
    sources = (
        lax.dot_general(table, select, (((0,), (1,)), ((), ())), preferred_element_type=jnp.float32)
        .astype(jnp.bfloat16)
        .reshape(coef_count, local_channels, slab_size)
    )
    turned = rotate_forward(compact_t, scaling, sources)
    mixed = convolve(turned, weight_zero, weight_one, weight_two)
    selector = (jnp.arange(local_nodes, dtype=jnp.int32)[:, None] == target_slot[None, :]).astype(
        jnp.bfloat16
    )
    listing = row_offsets()
    sums = []
    for degree in range(LMAX + 1):
        span = 2 * degree + 1
        picked_rows = [
            (row, offset)
            for row, (row_degree, offset) in enumerate(listing)
            if row_degree == degree
        ]
        left = jnp.concatenate(
            [
                (compact_t[offset : offset + span][None] * selector[:, None]).reshape(
                    local_nodes * span, slab_size
                )
                for row, offset in picked_rows
            ],
            axis=1,
        )
        right = jnp.concatenate([mixed[row] for row, offset in picked_rows], axis=0)
        sums.append(
            jnp.dot(left, right, preferred_element_type=jnp.float32).reshape(local_nodes, span, -1)
        )
    partial = jnp.concatenate(sums, axis=1).astype(jnp.bfloat16)
    return lax.psum_scatter(partial, "chan", scatter_dimension=2, tiled=True)


def solution(mesh):
    in_specs = (
        P("edge", None, "chan"),
        P(None, ("edge", "chan")),
        P("edge", None),
        P("edge"),
        P("edge"),
        P("edge"),
        P(None, "chan", None, None),
        P(None, None, "chan", None, None),
        P(None, None, "chan", None, None),
    )
    out_specs = P("edge", None, "chan")
    return jax.shard_map(shards, mesh=mesh, in_specs=in_specs, out_specs=out_specs, check_vma=False)
```

profile of v0, /device:TPU:1, one launch (start us, length us, event | category | flops | bytes accessed | tf_op | source)
XLA Modules:
  0.0 408.8 jit_solution(11529215945910362788)
XLA Ops:
  20.3 2.1 concatenate.68
  22.4 10.5 %all_gather.6 = bf16[512,236]{0,1:T(8,128)(2,1)S(1)} all-gather(bf16[128,236]{0,1:T(8,128)(2,1)S(1)} %concatenate.68), channel_id=1, replica_groups=mesh['edge'=64,'chan'=4] {'chan'}, dimensions={0}, use_global_device_ids=true | all-gather | bytes 302080 | tf_op jit(solution)/shard_map/all_gather | solution.py:185
  35.3 1.8 copy.63
  37.2 1.7 copy.54
  41.3 1.7 copy.61
  44.0 1.7 mul.5643
  45.7 1.7 mul.5646
  50.6 1.7 mul.5627
  52.3 1.7 mul.5630
  57.2 1.7 mul.5611
  58.9 1.7 mul.5614
  61.6 1.6 mul.5595
  63.2 1.6 mul.5598
  64.8 1.6 mul.5601
  67.3 1.6 mul.5199
  68.9 1.6 mul.5202
  70.5 1.6 mul.5205
  85.1 1.7 constant_dynamic-update-slice_fusion.60
  86.8 1.5 constant_dynamic-update-slice_fusion.59
  104.1 173.3 %all-gather.2.cloned.1.call-done = bf16[1024,3136]{1,0:T(8,128)(2,1)} async-done(((bf16[16,3136]{1,0:T(8,128)(2,1)}), bf16[1024,3136]{1,0:T(8,128)(2,1)}) %all-gather.2.cloned.1.call-update) | async-done | bytes 6422544 | tf_op jit(solution)/shard_map/all_gather | solution.py:182
  277.4 8.6 %fusion = bf16[3136,512]{1,0:T(8,128)(2,1)S(1)} fusion(bf16[1024,3136]{1,0:T(8,128)(2,1)} %all-gather.2.cloned.1.call-done, s32[512]{0:T(512)} %add.1082), kind=kOutput, calls=%fused_computation.1 | convolution fusion | flops 3290464256 | bytes 9635840 | tf_op jit(solution)/shard_map/dot_general | solution.py:192
  312.5 2.0 convolution_convert_fusion.6
  323.8 2.1 reshape.3360
  325.8 73.7 %reduce-scatter.4.cloned.1.call-done = bf16[64,784]{1,0:T(8,128)(2,1)} async-done(((bf16[256,784]{1,0:T(8,128)(2,1)}), bf16[64,784]{1,0:T(8,128)(2,1)}) %reduce-scatter.4.cloned.1.call-update) | async-done | bytes 100368
  (680 shorter events, 90.3 us)
Async XLA Ops:
  6.5 6.0 %copy-start.34 = (f32[98,7]{1,0:T(8,128)S(1)}, f32[98,7]{1,0:T(8,128)}, u32[]{:S(2)}) copy-start(f32[98,7]{1,0:T(8,128)} %constant.140.clone) | copy-start | bytes 8236
  6.5 6.5 %copy-start.13 = (f32[98,5]{1,0:T(8,128)S(1)}, f32[98,5]{1,0:T(8,128)}, u32[]{:S(2)}) copy-start(f32[98,5]{1,0:T(8,128)} %constant.139.clone) | copy-start | bytes 5884
  6.5 7.5 %copy-start.29 = (f32[98,3]{1,0:T(8,128)S(1)}, f32[98,3]{1,0:T(8,128)}, u32[]{:S(2)}) copy-start(f32[98,3]{1,0:T(8,128)} %constant.138.clone) | copy-start | bytes 3532
  6.5 270.9 %all-gather.2.cloned.1.call-start = ((), (), s32[]{:S(2)}) async-start(), calls=%async_computation.1 | async-start | bytes 6656000 | tf_op jit(solution)/shard_map/all_gather | solution.py:182
  8.4 6.9 %copy-start.240 = (f32[98,13]{1,0:T(8,128)S(1)}, f32[98,13]{1,0:T(8,128)}, u32[]{:S(2)}) copy-start(f32[98,13]{1,0:T(8,128)} %constant.143.clone) | copy-start | bytes 15292
  8.4 391.1 %reduce-scatter.4.cloned.1.call-start = ((), (), s32[]{:S(2)}) async-start(), calls=%async_computation.2 | async-start | bytes 573440
  18.6 15.5 %copy-start.9 = (bf16[2,5,64,5,256]{4,2,3,1,0:T(8,128)(2,1)S(1)}, bf16[2,5,64,5,256]{4,2,3,1,0:T(8,128)(2,1)}, u32[]{:S(2)}) copy-start(bf16[2,5,64,5,256]{4,2,3,1,0:T(8,128)(2,1)} %param.49) | copy-start | bytes 4915204
  72.7 15.7 %copy-start.30 = (bf16[112,512]{1,0:T(8,128)(2,1)S(1)}, bf16[112,512]{1,0:T(8,128)(2,1)}, u32[]{:S(2)}) copy-start(bf16[112,512]{1,0:T(8,128)(2,1)} %mul.5601) | copy-start | bytes 344068
  73.4 17.0 %copy-start.27 = (bf16[144,512]{1,0:T(8,128)(2,1)S(1)}, bf16[144,512]{1,0:T(8,128)(2,1)}, u32[]{:S(2)}) copy-start(bf16[144,512]{1,0:T(8,128)(2,1)} %mul.5611) | copy-start | bytes 442372
  85.1 4.7 %copy-start.25 = (bf16[80,2560]{1,0:T(8,128)(2,1)}, bf16[80,2560]{1,0:T(8,128)(2,1)S(1)}, u32[]{:S(2)}) copy-start(bf16[80,2560]{1,0:T(8,128)(2,1)S(1)} %constant_dynamic-update-slice_fusion.31) | copy-start | bytes 1228804
  85.1 6.4 %copy-start.23 = (bf16[176,512]{1,0:T(8,128)(2,1)S(1)}, bf16[176,512]{1,0:T(8,128)(2,1)}, u32[]{:S(2)}) copy-start(bf16[176,512]{1,0:T(8,128)(2,1)} %mul.5627) | copy-start | bytes 540676
  91.5 4.5 %copy-start.14 = (bf16[144,2560]{1,0:T(8,128)(2,1)}, bf16[144,2560]{1,0:T(8,128)(2,1)S(1)}, u32[]{:S(2)}) copy-start(bf16[144,2560]{1,0:T(8,128)(2,1)S(1)} %constant_dynamic-update-slice_fusion.61) | copy-start | bytes 2211844
  104.0 182.1 %copy-start.185 = (f32[1,512]{1,0:T(1,128)S(1)}, f32[1,512]{1,0:T(1,128)}, u32[]{:S(2)}) copy-start(f32[1,512]{1,0:T(1,128)} %get-tuple-element.152) | copy-start | bytes 6148
  104.0 182.1 %copy-start.186 = (f32[1,512]{1,0:T(1,128)S(1)}, f32[1,512]{1,0:T(1,128)}, u32[]{:S(2)}) copy-start(f32[1,512]{1,0:T(1,128)} %get-tuple-element.153) | copy-start | bytes 6148
  104.0 182.1 %copy-start.187 = (f32[1,512]{1,0:T(1,128)S(1)}, f32[1,512]{1,0:T(1,128)}, u32[]{:S(2)}) copy-start(f32[1,512]{1,0:T(1,128)} %get-tuple-element.154) | copy-start | bytes 6148
  104.0 182.1 %copy-start.188 = (f32[1,512]{1,0:T(1,128)S(1)}, f32[1,512]{1,0:T(1,128)}, u32[]{:S(2)}) copy-start(f32[1,512]{1,0:T(1,128)} %get-tuple-element.155) | copy-start | bytes 6148
  104.0 182.1 %copy-start.189 = (f32[1,512]{1,0:T(1,128)S(1)}, f32[1,512]{1,0:T(1,128)}, u32[]{:S(2)}) copy-start(f32[1,512]{1,0:T(1,128)} %get-tuple-element.156) | copy-start | bytes 6148
  104.0 182.4 %copy-start.162 = (f32[1,512]{1,0:T(1,128)S(1)}, f32[1,512]{1,0:T(1,128)}, u32[]{:S(2)}) copy-start(f32[1,512]{1,0:T(1,128)} %get-tuple-element.148) | copy-start | bytes 6148
  104.1 182.4 %copy-start.163 = (f32[1,512]{1,0:T(1,128)S(1)}, f32[1,512]{1,0:T(1,128)}, u32[]{:S(2)}) copy-start(f32[1,512]{1,0:T(1,128)} %get-tuple-element.149) | copy-start | bytes 6148
  104.1 182.4 %copy-start.164 = (f32[1,512]{1,0:T(1,128)S(1)}, f32[1,512]{1,0:T(1,128)}, u32[]{:S(2)}) copy-start(f32[1,512]{1,0:T(1,128)} %get-tuple-element.150) | copy-start | bytes 6148
  104.1 182.4 %copy-start.165 = (f32[1,512]{1,0:T(1,128)S(1)}, f32[1,512]{1,0:T(1,128)}, u32[]{:S(2)}) copy-start(f32[1,512]{1,0:T(1,128)} %get-tuple-element.151) | copy-start | bytes 6148
  277.4 9.1 %copy-start.197 = (f32[1,512]{1,0:T(1,128)S(1)}, f32[1,512]{1,0:T(1,128)}, u32[]{:S(2)}) copy-start(f32[1,512]{1,0:T(1,128)} %get-tuple-element.144) | copy-start | bytes 6148
  277.4 9.1 %copy-start.198 = (f32[1,512]{1,0:T(1,128)S(1)}, f32[1,512]{1,0:T(1,128)}, u32[]{:S(2)}) copy-start(f32[1,512]{1,0:T(1,128)} %get-tuple-element.145) | copy-start | bytes 6148
  277.4 9.1 %copy-start.199 = (f32[1,512]{1,0:T(1,128)S(1)}, f32[1,512]{1,0:T(1,128)}, u32[]{:S(2)}) copy-start(f32[1,512]{1,0:T(1,128)} %get-tuple-element.146) | copy-start | bytes 6148
  (219 other events, 358.4 us)
Sparse Core Ops, SparseCore 0:
  9.1 268.2 all-gather.1
  326.0 73.5 reduce-scatter.3
where the time goes:
time: 410 us; the launch traced here: 409 us
  waiting for transfers between devices  247 us (60%)
  local copies, waits for them, and re-layouts  75.8 us (18%)
  matrix products  30.5 us (7%)
  other arithmetic  26.9 us (7%)
  between operations  18.1 us (4%)
  blocking collectives  10.5 us (3%)
    all_gather x1, waiting for transfers between devices, shards(): table = lax.all_gather(node_flat, 'edge', axis=0, tiled=True)  173 us
    unnamed x3, waiting for transfers between devices  73.7 us
    unnamed x534, local copies, waits for them, and re-layouts  36.1 us
    mul x28, local copies, waits for them, and re-layouts, shards(): compact_t[offset:offset + span][None] * selector[:, None]  30.4 us
    all_gather x1, blocking collectives, shards(): packed_t = lax.all_gather(packed, 'chan', axis=0, tiled=True).T  10.5 us
    mul x14, other arithmetic, rotate_forward(): compact_t[offset + inner].astype(jnp.float32)[None, :]  9.2 us
    dot_general x1, matrix products, shards(): lax.dot_general(table, select, (((0,), (1,)), ((), ())), preferred_elemen...  8.62 us
  transfers between devices with their start and end apart: 2, of which 2 were waited for; matrix products, arithmetic and copies ran while one was open for 20% of the time, Pallas kernels for 0%

commit v1 on v0

--- a/solution.py
+++ b/solution.py
@@ -179,7 +179,8 @@
     coef_count = node_states.shape[1]
     group_count = lax.axis_size("edge")
     node_flat = node_states.reshape(local_nodes, coef_count * local_channels)
-    table = lax.all_gather(node_flat, "edge", axis=0, tiled=True)
+    repeated = jnp.stack([node_flat] * lax.axis_size("edge"))
+    table = jnp.concatenate(lax.all_to_all(repeated, "edge", 0, 0), axis=0)
     quarter, quarter_fade = wigner_rows(edge_vectors)
     packed = jnp.concatenate([quarter, quarter_fade[:, None]], axis=1).astype(jnp.bfloat16)
     packed_t = lax.all_gather(packed, "chan", axis=0, tiled=True).T

time: 410 us -> 262 us (0.64)
  waiting for transfers between devices: 247 us -> 87.2 us
  starting transfers between devices: 0.04 us -> 14 us
    all_gather x1 -> x0, waiting for transfers between devices: 173 us -> none  [shards(): table = lax.all_gather(node_flat, 'edge', axis=0, tiled=True)]
    all_to_all x0 -> x1, waiting for transfers between devices: none -> 53.7 us  [shards(): table = jnp.concatenate(lax.all_to_all(repeated, 'edge', 0, 0), axis=0)]
    unnamed x3 -> x2, waiting for transfers between devices: 73.7 us -> 33.5 us
    all_to_all x0 -> x1, starting transfers between devices: none -> 13.9 us  [shards(): table = jnp.concatenate(lax.all_to_all(repeated, 'edge', 0, 0), axis=0)]
    unnamed x534 -> x538, local copies, waits for them, and re-layouts: 36.1 us -> 36.1 us
  transfers between devices with their start and end apart: 2 -> 2, of which waited for: 2 -> 2; matrix products, arithmetic and copies ran while one was open for 20% -> 30% of each run, Pallas kernels for 0% -> 0%
where the time goes in v1:
time: 262 us; the launch traced here: 260 us
  waiting for transfers between devices  87.2 us (33%)
  local copies, waits for them, and re-layouts  78.4 us (30%)
  matrix products  29.8 us (11%)
  other arithmetic  24.1 us (9%)
  between operations  18.1 us (7%)
  starting transfers between devices  14 us (5%)
  blocking collectives  8.55 us (3%)
    all_to_all x1, waiting for transfers between devices, shards(): table = jnp.concatenate(lax.all_to_all(repeated, 'edge', 0, 0), axis=0)  53.7 us
    unnamed x538, local copies, waits for them, and re-layouts  36.1 us
    unnamed x2, waiting for transfers between devices  33.5 us
    mul x28, local copies, waits for them, and re-layouts, shards(): compact_t[offset:offset + span][None] * selector[:, None]  30.5 us
    all_to_all x1, starting transfers between devices, shards(): table = jnp.concatenate(lax.all_to_all(repeated, 'edge', 0, 0), axis=0)  13.9 us
    mul x14, other arithmetic, rotate_forward(): compact_t[offset + inner].astype(jnp.float32)[None, :]  9.25 us
    dot_general x1, matrix products, shards(): lax.dot_general(table, select, (((0,), (1,)), ((), ())), preferred_elemen...  8.64 us
    all_gather x1, blocking collectives, shards(): packed_t = lax.all_gather(packed, 'chan', axis=0, tiled=True).T  8.55 us
  transfers between devices with their start and end apart: 2, of which 2 were waited for; matrix products, arithmetic and copies ran while one was open for 30% of the time, Pallas kernels for 0%

profile of v1, /device:TPU:1, one launch (start us, length us, event | category | flops | bytes accessed | tf_op | source)
XLA Modules:
  0.0 260.1 jit_solution(2935120403479059129)
XLA Ops:
  7.7 3.2 %stack.24 = bf16[64,16,3136]{2,1,0:T(8,128)(2,1)} broadcast(bf16[16,3136]{1,0:T(8,128)(2,1)S(1)} %stack_reshape.2), dimensions={1,2} | broadcast | bytes 6522880 | tf_op jit(solution)/shard_map/stack | solution.py:182
  10.9 13.9 %all-to-all-start = ((bf16[64,16,3136]{2,1,0:T(8,128)(2,1)}), bf16[64,16,3136]{2,1,0:T(8,128)(2,1)}, u32[]{:S(2)}, u32[]{:S(2)}) async-start(bf16[64,16,3136]{2,1,0:T(8,128)(2,1)} %stack.24), calls=%async_computation | async-start | bytes 13107200 | tf_op jit(solution)/shard_map/all_to_all | solution.py:183
  33.4 2.1 concatenate.68
  35.5 8.5 %all_gather.3 = bf16[512,236]{0,1:T(8,128)(2,1)S(1)} all-gather(bf16[128,236]{0,1:T(8,128)(2,1)S(1)} %concatenate.68), channel_id=1, replica_groups=mesh['edge'=64,'chan'=4] {'chan'}, dimensions={0}, use_global_device_ids=true | all-gather | bytes 302080 | tf_op jit(solution)/shard_map/all_gather | solution.py:186
  46.4 1.8 copy.63
  48.4 1.7 copy.54
  52.5 1.7 copy.61
  55.1 1.7 mul.5643
  56.8 1.7 mul.5646
  61.8 1.7 mul.5627
  63.5 1.7 mul.5630
  68.4 1.7 mul.5611
  70.1 1.7 mul.5614
  72.8 1.6 mul.5595
  74.4 1.6 mul.5598
  76.0 1.6 mul.5601
  78.5 1.6 mul.5199
  80.0 1.6 mul.5202
  96.2 1.8 constant_dynamic-update-slice_fusion.60
  115.1 53.7 %all-to-all-done = bf16[64,16,3136]{2,1,0:T(8,128)(2,1)} async-done(((bf16[64,16,3136]{2,1,0:T(8,128)(2,1)}), bf16[64,16,3136]{2,1,0:T(8,128)(2,1)}, u32[]{:S(2)}, u32[]{:S(2)}) %all-to-all-start) | async-done | bytes 6422560 | tf_op jit(solution)/shard_map/all_to_all | solution.py:183
  169.0 8.6 %fusion = bf16[3136,512]{1,0:T(8,128)(2,1)S(1)} fusion(bf16[1024,3136]{1,0:T(8,128)(2,1)} %bitcast.23, s32[512]{0:T(512)} %add.1082), kind=kOutput, calls=%fused_computation.1 | convolution fusion | flops 3290464256 | bytes 9635840 | tf_op jit(solution)/shard_map/dot_general | solution.py:193
  204.0 2.0 convolution_convert_fusion.6
  215.3 2.1 reshape.3362
  217.4 33.4 %reduce-scatter.4.cloned.1.call-done = bf16[64,784]{1,0:T(8,128)(2,1)} async-done(((bf16[256,784]{1,0:T(8,128)(2,1)}), bf16[64,784]{1,0:T(8,128)(2,1)}) %reduce-scatter.4.cloned.1.call-update) | async-done | bytes 100368
  (684 shorter events, 89.3 us)
Async XLA Ops:
  10.9 14.0 %copy-start.38 = (f32[3,128]{1,0:T(4,128)S(1)}, f32[3,128]{1,0:T(4,128)}, u32[]{:S(2)}) copy-start(f32[3,128]{1,0:T(4,128)} %param.42) | copy-start | bytes 4612
  10.9 14.3 %copy-start.237 = (f32[3,98,1]{1,0,2:T(4,128)S(1)}, f32[3,98,1]{1,0,2:T(4,128)}, u32[]{:S(2)}) copy-start(f32[3,98,1]{1,0,2:T(4,128)} %constant.147) | copy-start | bytes 3532
  10.9 14.7 %copy-start.34 = (f32[98,7]{1,0:T(8,128)S(1)}, f32[98,7]{1,0:T(8,128)}, u32[]{:S(2)}) copy-start(f32[98,7]{1,0:T(8,128)} %constant.140.clone) | copy-start | bytes 8236
  10.9 15.2 %copy-start.13 = (f32[98,5]{1,0:T(8,128)S(1)}, f32[98,5]{1,0:T(8,128)}, u32[]{:S(2)}) copy-start(f32[98,5]{1,0:T(8,128)} %constant.139.clone) | copy-start | bytes 5884
  10.9 158.0 %all-to-all-start = ((bf16[64,16,3136]{2,1,0:T(8,128)(2,1)}), bf16[64,16,3136]{2,1,0:T(8,128)(2,1)}, u32[]{:S(2)}, u32[]{:S(2)}) async-start(bf16[64,16,3136]{2,1,0:T(8,128)(2,1)} %stack.24), calls=%async_computation | async-start | bytes 13107200 | tf_op jit(solution)/shard_map/all_to_all | solution.py:183
  24.9 226.0 %reduce-scatter.4.cloned.1.call-start = ((), (), s32[]{:S(2)}) async-start(), calls=%async_computation.2 | async-start | bytes 573440
  31.6 13.6 %copy-start.9 = (bf16[2,5,64,5,256]{4,2,3,1,0:T(8,128)(2,1)S(1)}, bf16[2,5,64,5,256]{4,2,3,1,0:T(8,128)(2,1)}, u32[]{:S(2)}) copy-start(bf16[2,5,64,5,256]{4,2,3,1,0:T(8,128)(2,1)} %param.49) | copy-start | bytes 4915204
  83.9 15.6 %copy-start.30 = (bf16[112,512]{1,0:T(8,128)(2,1)S(1)}, bf16[112,512]{1,0:T(8,128)(2,1)}, u32[]{:S(2)}) copy-start(bf16[112,512]{1,0:T(8,128)(2,1)} %mul.5601) | copy-start | bytes 344068
  84.5 16.9 %copy-start.27 = (bf16[144,512]{1,0:T(8,128)(2,1)S(1)}, bf16[144,512]{1,0:T(8,128)(2,1)}, u32[]{:S(2)}) copy-start(bf16[144,512]{1,0:T(8,128)(2,1)} %mul.5611) | copy-start | bytes 442372
  96.2 4.7 %copy-start.25 = (bf16[80,2560]{1,0:T(8,128)(2,1)}, bf16[80,2560]{1,0:T(8,128)(2,1)S(1)}, u32[]{:S(2)}) copy-start(bf16[80,2560]{1,0:T(8,128)(2,1)S(1)} %constant_dynamic-update-slice_fusion.31) | copy-start | bytes 1228804
  96.2 6.4 %copy-start.23 = (bf16[176,512]{1,0:T(8,128)(2,1)S(1)}, bf16[176,512]{1,0:T(8,128)(2,1)}, u32[]{:S(2)}) copy-start(bf16[176,512]{1,0:T(8,128)(2,1)} %mul.5627) | copy-start | bytes 540676
  102.6 4.5 %copy-start.14 = (bf16[144,2560]{1,0:T(8,128)(2,1)}, bf16[144,2560]{1,0:T(8,128)(2,1)S(1)}, u32[]{:S(2)}) copy-start(bf16[144,2560]{1,0:T(8,128)(2,1)S(1)} %constant_dynamic-update-slice_fusion.61) | copy-start | bytes 2211844
  168.9 8.8 %copy-start.186 = (f32[1,512]{1,0:T(1,128)S(1)}, f32[1,512]{1,0:T(1,128)}, u32[]{:S(2)}) copy-start(f32[1,512]{1,0:T(1,128)} %get-tuple-element.152) | copy-start | bytes 6148
  168.9 8.8 %copy-start.187 = (f32[1,512]{1,0:T(1,128)S(1)}, f32[1,512]{1,0:T(1,128)}, u32[]{:S(2)}) copy-start(f32[1,512]{1,0:T(1,128)} %get-tuple-element.153) | copy-start | bytes 6148
  168.9 8.8 %copy-start.188 = (f32[1,512]{1,0:T(1,128)S(1)}, f32[1,512]{1,0:T(1,128)}, u32[]{:S(2)}) copy-start(f32[1,512]{1,0:T(1,128)} %get-tuple-element.154) | copy-start | bytes 6148
  168.9 8.8 %copy-start.189 = (f32[1,512]{1,0:T(1,128)S(1)}, f32[1,512]{1,0:T(1,128)}, u32[]{:S(2)}) copy-start(f32[1,512]{1,0:T(1,128)} %get-tuple-element.155) | copy-start | bytes 6148
  168.9 8.8 %copy-start.190 = (f32[1,512]{1,0:T(1,128)S(1)}, f32[1,512]{1,0:T(1,128)}, u32[]{:S(2)}) copy-start(f32[1,512]{1,0:T(1,128)} %get-tuple-element.156) | copy-start | bytes 6148
  168.9 9.2 %copy-start.163 = (f32[1,512]{1,0:T(1,128)S(1)}, f32[1,512]{1,0:T(1,128)}, u32[]{:S(2)}) copy-start(f32[1,512]{1,0:T(1,128)} %get-tuple-element.148) | copy-start | bytes 6148
  168.9 9.2 %copy-start.164 = (f32[1,512]{1,0:T(1,128)S(1)}, f32[1,512]{1,0:T(1,128)}, u32[]{:S(2)}) copy-start(f32[1,512]{1,0:T(1,128)} %get-tuple-element.149) | copy-start | bytes 6148
  168.9 9.2 %copy-start.165 = (f32[1,512]{1,0:T(1,128)S(1)}, f32[1,512]{1,0:T(1,128)}, u32[]{:S(2)}) copy-start(f32[1,512]{1,0:T(1,128)} %get-tuple-element.150) | copy-start | bytes 6148
  168.9 9.2 %copy-start.166 = (f32[1,512]{1,0:T(1,128)S(1)}, f32[1,512]{1,0:T(1,128)}, u32[]{:S(2)}) copy-start(f32[1,512]{1,0:T(1,128)} %get-tuple-element.151) | copy-start | bytes 6148
  168.9 9.2 %copy-start.198 = (f32[1,512]{1,0:T(1,128)S(1)}, f32[1,512]{1,0:T(1,128)}, u32[]{:S(2)}) copy-start(f32[1,512]{1,0:T(1,128)} %get-tuple-element.144) | copy-start | bytes 6148
  168.9 9.2 %copy-start.199 = (f32[1,512]{1,0:T(1,128)S(1)}, f32[1,512]{1,0:T(1,128)}, u32[]{:S(2)}) copy-start(f32[1,512]{1,0:T(1,128)} %get-tuple-element.145) | copy-start | bytes 6148
  168.9 9.2 %copy-start.200 = (f32[1,512]{1,0:T(1,128)S(1)}, f32[1,512]{1,0:T(1,128)}, u32[]{:S(2)}) copy-start(f32[1,512]{1,0:T(1,128)} %get-tuple-element.146) | copy-start | bytes 6148
  (221 other events, 363.4 us)
Sparse Core Ops, SparseCore 0:
  217.5 33.2 reduce-scatter.3
